TPU v7x, 32 devices: a whole 2x2x4 slice. The times are simulated.
32 devices in a mesh: grp: 2 (over y), gx: 16 (over z, x, core), gy: 1.
Axes of the slice: x: 2, y: 2, z: 4, core: 2. Of those that a mesh axis runs over, the one named last changes fastest.
Arguments:
- residue_feats: bfloat16 [512, 256], P(('grp', 'gx')), parts along dimension 0, may hold values from -6 to 6
- pair_feats: bfloat16 [64, 512, 256], P(None, ('grp', 'gx'), 'gy'), parts along dimension 1, may hold values from -30 to 30
- w_row: bfloat16 [256, 64], replicated, may hold values from -0.375 to 0.375
- w_col: bfloat16 [256, 64], replicated, may hold values from -0.375 to 0.375
- first_taps: bfloat16 [9, 64, 64], replicated, may hold values from -0.25 to 0.25
- second_taps: bfloat16 [9, 64, 64], replicated, may hold values from -0.25 to 0.25
- norm_scale: float32 [2, 64], replicated, may hold values from 0.25 to 1.75
- norm_shift: float32 [2, 64], replicated, may hold values from -2 to 2
Outputs:
- symmetric: bfloat16 [64, 512, 256], P(None, ('grp', 'gx'), 'gy'), parts along dimension 1
There are 2 independent parts, one for each index of `grp`. A program takes and returns all parts, laid end to end along the dimension named above; an argument that names none is the same for every part. Nothing has to cross between parts.
All inputs are finite; a program needn't handle non-finite values.
Results may differ from a plain program's by a relative error of at most 0.012.
Values may be sent and summed in bfloat16 or wider, within the bound.
A program may use at most 64 MiB of HBM per device.

v0:
```python
import jax
import jax.numpy as jnp
from jax import lax
from jax.sharding import PartitionSpec as P

DILATION_STEP = 8
epsilon = 1e-05


def with_halo(cells, sides, width):
    for axis, dim in sides:
        count = lax.axis_size(axis)
        ends = count - 1
        head = lax.slice_in_dim(cells, 0, width, axis=dim)
        tail = lax.slice_in_dim(cells, cells.shape[dim] - width, cells.shape[dim], axis=dim)
        cells = jnp.concatenate(
            [
                lax.ppermute(tail, axis, [(i, (i + 1) % count) for i in range(ends)]),
                cells,
                lax.ppermute(head, axis, [((i + 1) % count, i) for i in range(ends)]),
            ],
            axis=dim,
        )
    return cells


def dilated(receptive_region, weights):
    row_count = receptive_region.shape[1]
    col_count = receptive_region.shape[2]
    border_padded_input = with_halo(receptive_region, (("gx", 1), ("gy", 2)), DILATION_STEP)
    tap_sum_total = jnp.zeros((weights.shape[1], row_count, col_count), jnp.float32)
    for filter_tap_index in range(9):
        row_displacement = filter_tap_index // 3 * DILATION_STEP
        column_displacement = filter_tap_index % 3 * DILATION_STEP
        window = border_padded_input[
            :,
            row_displacement : row_displacement + row_count,
            column_displacement : column_displacement + col_count,
        ]
        tap_sum_total = tap_sum_total + jnp.einsum(
            "oc,crw->orw", weights[filter_tap_index], window, preferred_element_type=jnp.float32
        )
    return tap_sum_total


def normalized(tap_sum_total, gain, shift):
    cell_count = (
        tap_sum_total.shape[1] * tap_sum_total.shape[2] * lax.axis_size("gx") * lax.axis_size("gy")
    )
    first_sum, second_sum = lax.psum(
        (jnp.sum(tap_sum_total, axis=(1, 2)), jnp.sum(tap_sum_total * tap_sum_total, axis=(1, 2))),
        ("gx", "gy"),
    )
    average = first_sum / cell_count
    spread = second_sum / cell_count - average * average
    centred = tap_sum_total - average[:, None, None]
    factor = gain * lax.rsqrt(spread + epsilon)
    return centred * factor[:, None, None] + shift[:, None, None]


def body(residue_feats, pair_feats, w_row, w_col, first_taps, second_taps, norm_scale, norm_shift):
    col_count = pair_feats.shape[2]
    col_start = lax.axis_index("gy") * col_count
    row_part = jnp.dot(residue_feats, w_row, preferred_element_type=jnp.float32).astype(
        jnp.bfloat16
    )
    everyone = lax.all_gather(residue_feats, "gx", axis=0, tiled=True)
    col_feats = lax.dynamic_slice_in_dim(everyone, col_start, col_count, 0)
    col_part = jnp.dot(col_feats, w_col, preferred_element_type=jnp.float32).astype(jnp.bfloat16)
    block_in = (
        pair_feats.astype(jnp.float32)
        + row_part.T.astype(jnp.float32)[:, :, None]
        + col_part.T.astype(jnp.float32)[:, None, :]
    ).astype(jnp.bfloat16)
    first_conv = dilated(block_in, first_taps)
    activated = jax.nn.elu(normalized(first_conv, norm_scale[0], norm_shift[0])).astype(
        jnp.bfloat16
    )
    second_conv = dilated(activated, second_taps)
    block_out = jax.nn.elu(
        block_in.astype(jnp.float32) + normalized(second_conv, norm_scale[1], norm_shift[1])
    ).astype(jnp.bfloat16)
    whole_rows = lax.all_gather(block_out, "gy", axis=2, tiled=True)
    columns = lax.all_to_all(whole_rows, "gx", split_axis=2, concat_axis=1, tiled=True)
    flipped = lax.dynamic_slice_in_dim(columns, col_start, col_count, 1)
    mirrored = jnp.transpose(flipped, (0, 2, 1))
    return (0.5 * (block_out.astype(jnp.float32) + mirrored.astype(jnp.float32))).astype(
        jnp.bfloat16
    )


def solution(mesh):
    placed = (P(("grp", "gx"), None), P(None, ("grp", "gx"), "gy"), P(), P(), P(), P(), P(), P())
    return jax.shard_map(
        body, mesh=mesh, in_specs=placed, out_specs=P(None, ("grp", "gx"), "gy"), check_vma=False
    )
```

profile of v0, /device:TPU:0, one launch (start us, length us, event | category | flops | bytes accessed | tf_op | source)
XLA Modules:
  0.0 140.1 jit_solution(18333366935052121485)
XLA Ops:
  0.0 23.8 %all_gather.4 = bf16[256,256]{1,0:T(8,128)(2,1)S(1)} all-gather(bf16[16,256]{1,0:T(8,128)(2,1)} %param.8), channel_id=1, replica_groups=mesh['grp'=2,'gx'=16,'gy'=1] {'gx'}, dimensions={0}, use_global_device_ids=true | all-gather | bytes 139264 | tf_op jit(solution)/shard_map/all_gather | solution.py:67
  23.8 0.9 fusion.13
  24.9 1.3 add_convert_fusion
  26.2 2.3 %collective-permute-start = (bf16[64,8,256]{2,0,1:T(8,128)(2,1)S(1)}, bf16[64,8,256]{2,0,1:T(8,128)(2,1)S(1)}, u32[]{:S(2)}, u32[]{:S(2)}) collective-permute-start(bf16[64,8,256]{2,0,1:T(8,128)(2,1)S(1)} %get-tuple-element.23), channel_id=1, source_target_pairs={{0,1},{1,2},{2,3},{3,4},{4,5},{5,6},{6,7},{7,8},{8,9},{9,10},{10,1... | collective-permute-start | bytes 786440 | tf_op jit(solution)/shard_map/ppermute | solution.py:18
  28.5 1.3 collective-permute-start.1
  30.1 1.8 %collective-permute-done.1 = bf16[64,8,256]{2,0,1:T(8,128)(2,1)S(1)} collective-permute-done((bf16[64,8,256]{2,0,1:T(8,128)(2,1)S(1)}, bf16[64,8,256]{2,0,1:T(8,128)(2,1)S(1)}, u32[]{:S(2)}, u32[]{:S(2)}) %collective-permute-start.1) | collective-permute-done | bytes 262176 | tf_op jit(solution)/shard_map/ppermute | solution.py:20
  32.3 0.7 collective-permute-start.2
  33.0 0.7 collective-permute-start.3
  34.3 1.3 maximum_maximum_fusion
  38.0 33.9 %all-reduce.1 = (f32[64]{0:T(128)S(1)}, f32[64]{0:T(128)S(1)}) all-reduce(f32[64]{0:T(128)S(1)} %get-tuple-element.8, f32[64]{0:T(128)S(1)} %get-tuple-element.7), channel_id=1, replica_groups=mesh['grp'=2,'gx'=16,'gy'=1] {'gx','gy'}, use_global_device_ids=true, to_apply=%region_3.0 | all-reduce | flops 128 | bytes 1024 | tf_op jit(solution)/shard_map/psum | solution.py:50
  72.6 1.3 collective-permute-start.4
  73.9 1.3 collective-permute-start.5
  75.5 1.8 %collective-permute-done.5 = bf16[64,8,256]{2,0,1:T(8,128)(2,1)S(1)} collective-permute-done((bf16[64,8,256]{2,0,1:T(8,128)(2,1)S(1)}, bf16[64,8,256]{2,0,1:T(8,128)(2,1)S(1)}, u32[]{:S(2)}, u32[]{:S(2)}) %collective-permute-start.5) | collective-permute-done | bytes 262176 | tf_op jit(solution)/shard_map/ppermute | solution.py:20
  77.8 0.7 collective-permute-start.6
  78.5 0.7 collective-permute-start.7
  79.7 1.3 maximum_maximum_fusion.1
  83.4 31.5 %all-reduce = (f32[64]{0:T(128)S(1)}, f32[64]{0:T(128)S(1)}) all-reduce(f32[64]{0:T(128)S(1)} %get-tuple-element.6, f32[64]{0:T(128)S(1)} %get-tuple-element.5), channel_id=1, replica_groups=mesh['grp'=2,'gx'=16,'gy'=1] {'gx','gy'}, use_global_device_ids=true, to_apply=%region_7.8 | all-reduce | flops 128 | bytes 1024 | tf_op jit(solution)/shard_map/psum | solution.py:50
  115.0 0.7 fusion.17
  115.7 1.0 copy.18
  116.7 0.7 reshape.32
  117.4 16.9 %all_to_all.4 = bf16[16,2,8192]{2,1,0:T(2,128)(2,1)S(1)} all-to-all(bf16[16,2,8192]{2,1,0:T(2,128)(2,1)S(1)} %reshape.32), channel_id=1, replica_groups=mesh['grp'=2,'gx'=16,'gy'=1] {'gx'}, dimensions={0} | all-to-all | bytes 1048576 | tf_op jit(solution)/shard_map/all_to_all | solution.py:84
  135.7 2.0 %copy.21 = f32[64,256,16]{1,0,2:T(8,128)} copy(f32[64,256,16]{0,2,1:T(8,128)S(1)} %bitcast.109) | data formatting | bytes 2097152 | tf_op jit(solution)/shard_map/convert_element_type | solution.py:87
  137.6 1.4 fusion.19
  139.0 1.1 copy.22
  (51 shorter events, 9.4 us)
Async XLA Ops:
  0.0 24.7 %copy-start = (bf16[256,64]{0,1:T(8,128)(2,1)S(1)}, bf16[256,64]{0,1:T(8,128)(2,1)}, u32[]{:S(2)}) copy-start(bf16[256,64]{0,1:T(8,128)(2,1)} %param.11) | copy-start | bytes 98308
  0.0 29.8 %copy-start.5 = (f32[2,64]{1,0:T(2,128)S(1)}, f32[2,64]{1,0:T(2,128)}, u32[]{:S(2)}) copy-start(f32[2,64]{1,0:T(2,128)} %param.15) | copy-start | bytes 1540
  0.0 29.8 %copy-start.2 = (bf16[9,64,64]{2,1,0:T(8,128)(2,1)S(1)}, bf16[9,64,64]{2,1,0:T(8,128)(2,1)}, u32[]{:S(2)}) copy-start(bf16[9,64,64]{2,1,0:T(8,128)(2,1)} %param.12) | copy-start | bytes 221188
  26.2 3.9 %collective-permute-start = (bf16[64,8,256]{2,0,1:T(8,128)(2,1)S(1)}, bf16[64,8,256]{2,0,1:T(8,128)(2,1)S(1)}, u32[]{:S(2)}, u32[]{:S(2)}) collective-permute-start(bf16[64,8,256]{2,0,1:T(8,128)(2,1)S(1)} %get-tuple-element.23), channel_id=1, source_target_pairs={{0,1},{1,2},{2,3},{3,4},{4,5},{5,6},{6,7},{7,8},{8,9},{9,10},{10,1... | collective-permute-start | bytes 786440 | tf_op jit(solution)/shard_map/ppermute | solution.py:18
  28.5 3.4 %collective-permute-start.1 = (bf16[64,8,256]{2,0,1:T(8,128)(2,1)S(1)}, bf16[64,8,256]{2,0,1:T(8,128)(2,1)S(1)}, u32[]{:S(2)}, u32[]{:S(2)}) collective-permute-start(bf16[64,8,256]{2,0,1:T(8,128)(2,1)S(1)} %get-tuple-element.24), channel_id=1, source_target_pairs={{1,0},{2,1},{3,2},{4,3},{5,4},{6,5},{7,6},{8,7},{9,8},{10,9},{11,1... | collective-permute-start | bytes 786440 | tf_op jit(solution)/shard_map/ppermute | solution.py:20
  32.3 1.9 %collective-permute-start.2 = (bf16[64,32,8]{2,0,1:T(8,128)(2,1)S(1)}, bf16[64,32,8]{2,0,1:T(8,128)(2,1)S(1)}, u32[]{:S(2)}, u32[]{:S(2)}) collective-permute-start(bf16[64,32,8]{2,0,1:T(8,128)(2,1)S(1)} %get-tuple-element.19), channel_id=1, source_target_pairs={} | collective-permute-start | bytes 98312 | tf_op jit(solution)/shard_map/ppermute | solution.py:18
  33.0 1.3 collective-permute-start.3
  37.3 34.6 %copy-start.4 = (f32[2,64]{1,0:T(2,128)S(1)}, f32[2,64]{1,0:T(2,128)}, u32[]{:S(2)}) copy-start(f32[2,64]{1,0:T(2,128)} %param.14) | copy-start | bytes 1540
  38.0 37.2 %copy-start.3 = (bf16[9,64,64]{2,1,0:T(8,128)(2,1)S(1)}, bf16[9,64,64]{2,1,0:T(8,128)(2,1)}, u32[]{:S(2)}) copy-start(bf16[9,64,64]{2,1,0:T(8,128)(2,1)} %param.13) | copy-start | bytes 221188
  72.6 2.9 %collective-permute-start.4 = (bf16[64,8,256]{2,0,1:T(8,128)(2,1)S(1)}, bf16[64,8,256]{2,0,1:T(8,128)(2,1)S(1)}, u32[]{:S(2)}, u32[]{:S(2)}) collective-permute-start(bf16[64,8,256]{2,0,1:T(8,128)(2,1)S(1)} %get-tuple-element.21), channel_id=1, source_target_pairs={{0,1},{1,2},{2,3},{3,4},{4,5},{5,6},{6,7},{7,8},{8,9},{9,10},{10,1... | collective-permute-start | bytes 786440 | tf_op jit(solution)/shard_map/ppermute | solution.py:18
  73.9 3.4 %collective-permute-start.5 = (bf16[64,8,256]{2,0,1:T(8,128)(2,1)S(1)}, bf16[64,8,256]{2,0,1:T(8,128)(2,1)S(1)}, u32[]{:S(2)}, u32[]{:S(2)}) collective-permute-start(bf16[64,8,256]{2,0,1:T(8,128)(2,1)S(1)} %get-tuple-element.22), channel_id=1, source_target_pairs={{1,0},{2,1},{3,2},{4,3},{5,4},{6,5},{7,6},{8,7},{9,8},{10,9},{11,1... | collective-permute-start | bytes 786440 | tf_op jit(solution)/shard_map/ppermute | solution.py:20
  77.8 1.9 %collective-permute-start.6 = (bf16[64,32,8]{2,0,1:T(8,128)(2,1)S(1)}, bf16[64,32,8]{2,0,1:T(8,128)(2,1)S(1)}, u32[]{:S(2)}, u32[]{:S(2)}) collective-permute-start(bf16[64,32,8]{2,0,1:T(8,128)(2,1)S(1)} %get-tuple-element.15), channel_id=1, source_target_pairs={} | collective-permute-start | bytes 98312 | tf_op jit(solution)/shard_map/ppermute | solution.py:18
  78.5 1.3 collective-permute-start.7
  82.7 32.2 %copy-start.1 = (bf16[64,16,256]{2,1,0:T(8,128)(2,1)S(1)}, bf16[64,16,256]{2,1,0:T(8,128)(2,1)}, u32[]{:S(2)}) copy-start(bf16[64,16,256]{2,1,0:T(8,128)(2,1)} %param.9) | copy-start | bytes 1572868
where the time goes:
time: 141 us; the launch traced here: 140 us
  blocking collectives  106 us (75%)
  starting transfers between devices  8.9 us (6%)
  matrix products  7.38 us (5%)
  other arithmetic  7.08 us (5%)
  local copies, waits for them, and re-layouts  6.52 us (5%)
  waiting for transfers between devices  3.66 us (3%)
    psum x2, blocking collectives, normalized(): lax.psum((jnp.sum(tap_sum_total, axis=(1, 2)), jnp.sum(tap_sum_total * ta...  65.5 us
    all_gather x1, blocking collectives, body(): everyone = lax.all_gather(residue_feats, 'gx', axis=0, tiled=True)  23.8 us
    all_to_all x1, blocking collectives, body(): lax.all_to_all(whole_rows, 'gx', split_axis=2, concat_axis=1, tiled=True)  16.9 us
    dot_general x18, matrix products, dilated(): jnp.einsum('oc,crw->orw', weights[filter_tap_index], window, preferred_el...  6.34 us
    ppermute x4, starting transfers between devices, with_halo(): lax.ppermute(tail, axis, [(i, (i + 1) % count) for i in range(ends)])  4.94 us
    ppermute x4, starting transfers between devices, with_halo(): lax.ppermute(head, axis, [((i + 1) % count, i) for i in range(ends)])  3.96 us
    ppermute x4, waiting for transfers between devices, with_halo(): lax.ppermute(head, axis, [((i + 1) % count, i) for i in range(ends)])  3.65 us
    concatenate x4, other arithmetic, with_halo(): jnp.concatenate([lax.ppermute(tail, axis, [(i, (i + 1) % count) for i in...  2.87 us
  transfers between devices with their start and end apart: 8, of which 2 were waited for; matrix products, arithmetic and copies ran while one was open for 1% of the time, Pallas kernels for 0%

commit v1 on v0

--- a/solution.py
+++ b/solution.py
@@ -5,6 +5,28 @@
 
 DILATION_STEP = 8
 epsilon = 1e-05
+
+
+def laid_out(pieces, dim):
+    pieces = jnp.moveaxis(pieces, 0, dim)
+    dims = pieces.shape
+    return pieces.reshape(*dims[:dim], dims[dim] * dims[dim + 1], *dims[dim + 2 :])
+
+
+def collected_by_bits(array, axis):
+    size = lax.axis_size(axis)
+    blocks = array[None]
+    for level in range(size.bit_length() - 1):
+        bit = 1 << level
+        other = lax.ppermute(blocks, axis, [(i, i ^ bit) for i in range(size)])
+        both = jnp.stack([blocks, other])
+        upper = lax.axis_index(axis) >> level & 1
+        blocks = jnp.where(upper == 0, both, both[::-1]).reshape(-1, *array.shape)
+    return blocks
+
+
+def collect(x, axis, dim):
+    return laid_out(collected_by_bits(x, axis), dim)
 
 
 def with_halo(cells, sides, width):
@@ -64,7 +86,7 @@
     row_part = jnp.dot(residue_feats, w_row, preferred_element_type=jnp.float32).astype(
         jnp.bfloat16
     )
-    everyone = lax.all_gather(residue_feats, "gx", axis=0, tiled=True)
+    everyone = collect(residue_feats, "gx", 0)
     col_feats = lax.dynamic_slice_in_dim(everyone, col_start, col_count, 0)
     col_part = jnp.dot(col_feats, w_col, preferred_element_type=jnp.float32).astype(jnp.bfloat16)
     block_in = (

time: 141 us -> 135 us (0.957)
  blocking collectives: 106 us -> 84.7 us
  starting transfers between devices: 8.9 us -> 16.6 us
  waiting for transfers between devices: 3.66 us -> 11 us
    all_gather x1 -> x0, blocking collectives: 23.8 us -> none  [body(): everyone = lax.all_gather(residue_feats, 'gx', axis=0, tiled=True)]
    ppermute x0 -> x4, starting transfers between devices: none -> 8.64 us  [collected_by_bits(): other = lax.ppermute(blocks, axis, [(i, i ^ bit) for i in range(size)])]
    ppermute x0 -> x4, waiting for transfers between devices: none -> 5.26 us  [collected_by_bits(): other = lax.ppermute(blocks, axis, [(i, i ^ bit) for i in range(size)])]
    psum x2, blocking collectives: 65.5 us -> 67.6 us  [normalized(): lax.psum((jnp.sum(tap_sum_total, axis=(1, 2)), jnp.sum(tap_sum_total * ta...]
    ppermute x4, waiting for transfers between devices: 3.65 us -> 5.7 us  [with_halo(): lax.ppermute(head, axis, [((i + 1) % count, i) for i in range(ends)])]
  transfers between devices with their start and end apart: 8 -> 12, of which waited for: 2 -> 6; matrix products, arithmetic and copies ran while one was open for 1% -> 2% of each run, Pallas kernels for 0% -> 0%
where the time goes in v1:
time: 135 us; the launch traced here: 134 us
  blocking collectives  84.7 us (63%)
  starting transfers between devices  16.6 us (12%)
  waiting for transfers between devices  11 us (8%)
  matrix products  7.39 us (5%)
  local copies, waits for them, and re-layouts  7.27 us (5%)
  other arithmetic  6.84 us (5%)
    psum x2, blocking collectives, normalized(): lax.psum((jnp.sum(tap_sum_total, axis=(1, 2)), jnp.sum(tap_sum_total * ta...  67.6 us
    all_to_all x1, blocking collectives, body(): lax.all_to_all(whole_rows, 'gx', split_axis=2, concat_axis=1, tiled=True)  17.1 us
    ppermute x4, starting transfers between devices, collected_by_bits(): other = lax.ppermute(blocks, axis, [(i, i ^ bit) for i in range(size)])  8.64 us
    dot_general x18, matrix products, dilated(): jnp.einsum('oc,crw->orw', weights[filter_tap_index], window, preferred_el...  6.36 us
    ppermute x4, waiting for transfers between devices, with_halo(): lax.ppermute(head, axis, [((i + 1) % count, i) for i in range(ends)])  5.7 us
    ppermute x4, waiting for transfers between devices, collected_by_bits(): other = lax.ppermute(blocks, axis, [(i, i ^ bit) for i in range(size)])  5.26 us
    ppermute x4, starting transfers between devices, with_halo(): lax.ppermute(tail, axis, [(i, (i + 1) % count) for i in range(ends)])  3.99 us
    ppermute x4, starting transfers between devices, with_halo(): lax.ppermute(head, axis, [((i + 1) % count, i) for i in range(ends)])  3.96 us
  transfers between devices with their start and end apart: 12, of which 6 were waited for; matrix products, arithmetic and copies ran while one was open for 2% of the time, Pallas kernels for 0%

profile of v1, /device:TPU:0, one launch (start us, length us, event | category | flops | bytes accessed | tf_op | source)
XLA Modules:
  0.0 134.1 jit_solution(10449684957209514085)
XLA Ops:
  0.5 1.0 collective-permute-done
  2.2 2.9 %collective-permute-start.1 = (bf16[2,16,256]{2,1,0:T(8,128)(2,1)S(1)}, bf16[2,16,256]{2,1,0:T(8,128)(2,1)S(1)}, u32[]{:S(2)}, u32[]{:S(2)}) collective-permute-start(bf16[2,16,256]{2,1,0:T(8,128)(2,1)S(1)} %get-tuple-element.26), channel_id=1, source_target_pairs={{0,2},{1,3},{2,0},{3,1},{4,6},{5,7},{6,4},{7,5},{8,10},{9,11},{10,... | collective-permute-start | bytes 49160 | tf_op jit(solution)/shard_map/ppermute | solution.py:21
  5.1 1.7 %collective-permute-done.1 = bf16[2,16,256]{2,1,0:T(8,128)(2,1)S(1)} collective-permute-done((bf16[2,16,256]{2,1,0:T(8,128)(2,1)S(1)}, bf16[2,16,256]{2,1,0:T(8,128)(2,1)S(1)}, u32[]{:S(2)}, u32[]{:S(2)}) %collective-permute-start.1) | collective-permute-done | bytes 16416 | tf_op jit(solution)/shard_map/ppermute | solution.py:21
  6.9 2.2 %collective-permute-start.2 = (bf16[4,16,256]{2,1,0:T(8,128)(2,1)S(1)}, bf16[4,16,256]{2,1,0:T(8,128)(2,1)S(1)}, u32[]{:S(2)}, u32[]{:S(2)}) collective-permute-start(bf16[4,16,256]{2,1,0:T(8,128)(2,1)S(1)} %bitcast.133), channel_id=1, source_target_pairs={{0,4},{1,5},{2,6},{3,7},{4,0},{5,1},{6,2},{7,3},{8,12},{9,13},{10,... | collective-permute-start | bytes 98312 | tf_op jit(solution)/shard_map/ppermute | solution.py:21
  9.0 0.9 fusion.14
  9.9 1.0 collective-permute-done.2
  11.0 3.1 %collective-permute-start.3 = (bf16[8,16,256]{2,1,0:T(8,128)(2,1)S(1)}, bf16[8,16,256]{2,1,0:T(8,128)(2,1)S(1)}, u32[]{:S(2)}, u32[]{:S(2)}) collective-permute-start(bf16[8,16,256]{2,1,0:T(8,128)(2,1)S(1)} %bitcast.131), channel_id=1, source_target_pairs={{0,8},{1,9},{2,10},{3,11},{4,12},{5,13},{6,14},{7,15},{8,0},{9,1},... | collective-permute-start | bytes 196616 | tf_op jit(solution)/shard_map/ppermute | solution.py:21
  14.1 0.8 slice_bitcast_fusion
  14.8 1.5 %collective-permute-done.3 = bf16[8,16,256]{2,1,0:T(8,128)(2,1)S(1)} collective-permute-done((bf16[8,16,256]{2,1,0:T(8,128)(2,1)S(1)}, bf16[8,16,256]{2,1,0:T(8,128)(2,1)S(1)}, u32[]{:S(2)}, u32[]{:S(2)}) %collective-permute-start.3) | collective-permute-done | bytes 65568 | tf_op jit(solution)/shard_map/ppermute | solution.py:21
  16.8 1.3 collective-permute-start.4
  18.2 1.3 collective-permute-start.5
  19.8 3.9 %collective-permute-done.5 = bf16[64,8,256]{2,0,1:T(8,128)(2,1)S(1)} collective-permute-done((bf16[64,8,256]{2,0,1:T(8,128)(2,1)S(1)}, bf16[64,8,256]{2,0,1:T(8,128)(2,1)S(1)}, u32[]{:S(2)}, u32[]{:S(2)}) %collective-permute-start.5) | collective-permute-done | bytes 262176 | tf_op jit(solution)/shard_map/ppermute | solution.py:42
  26.0 1.3 maximum_maximum_fusion
  29.7 34.7 %all-reduce.1 = (f32[64]{0:T(128)S(1)}, f32[64]{0:T(128)S(1)}) all-reduce(f32[64]{0:T(128)S(1)} %get-tuple-element.8, f32[64]{0:T(128)S(1)} %get-tuple-element.7), channel_id=1, replica_groups=mesh['grp'=2,'gx'=16,'gy'=1] {'gx','gy'}, use_global_device_ids=true, to_apply=%region_3.4 | all-reduce | flops 128 | bytes 1024 | tf_op jit(solution)/shard_map/psum | solution.py:72
  65.1 1.3 collective-permute-start.8
  66.4 1.3 collective-permute-start.9
  68.0 1.8 %collective-permute-done.9 = bf16[64,8,256]{2,0,1:T(8,128)(2,1)S(1)} collective-permute-done((bf16[64,8,256]{2,0,1:T(8,128)(2,1)S(1)}, bf16[64,8,256]{2,0,1:T(8,128)(2,1)S(1)}, u32[]{:S(2)}, u32[]{:S(2)}) %collective-permute-start.9) | collective-permute-done | bytes 262176 | tf_op jit(solution)/shard_map/ppermute | solution.py:42
  72.2 1.3 maximum_maximum_fusion.1
  75.9 33.0 %all-reduce = (f32[64]{0:T(128)S(1)}, f32[64]{0:T(128)S(1)}) all-reduce(f32[64]{0:T(128)S(1)} %get-tuple-element.6, f32[64]{0:T(128)S(1)} %get-tuple-element.5), channel_id=1, replica_groups=mesh['grp'=2,'gx'=16,'gy'=1] {'gx','gy'}, use_global_device_ids=true, to_apply=%region_7.8 | all-reduce | flops 128 | bytes 1024 | tf_op jit(solution)/shard_map/psum | solution.py:72
  109.6 1.0 copy.18
  111.3 17.1 %all_to_all.4 = bf16[16,2,8192]{2,1,0:T(2,128)(2,1)S(1)} all-to-all(bf16[16,2,8192]{2,1,0:T(2,128)(2,1)S(1)} %reshape.44), channel_id=1, replica_groups=mesh['grp'=2,'gx'=16,'gy'=1] {'gx'}, dimensions={0} | all-to-all | bytes 1048576 | tf_op jit(solution)/shard_map/all_to_all | solution.py:106
  129.7 2.0 %copy.21 = f32[64,256,16]{1,0,2:T(8,128)} copy(f32[64,256,16]{0,2,1:T(8,128)S(1)} %bitcast.126) | data formatting | bytes 2097152 | tf_op jit(solution)/shard_map/convert_element_type | solution.py:109
  131.7 1.4 %fusion.20 = bf16[64,16,256]{2,0,1:T(8,128)(2,1)S(1)} fusion(f32[64,256,16]{1,0,2:T(8,128)} %copy.21, bf16[64,16,256]{2,0,1:T(8,128)(2,1)S(1)} %fusion.18), kind=kLoop, calls=%fused_computation.38 | loop fusion | flops 1048576 | bytes 2097152 | tf_op jit(solution)/shard_map/convert_element_type | solution.py:109
  133.1 1.1 copy.22
  (64 shorter events, 15.1 us)
Async XLA Ops:
  0.0 16.4 %copy-start = (bf16[256,64]{0,1:T(8,128)(2,1)S(1)}, bf16[256,64]{0,1:T(8,128)(2,1)}, u32[]{:S(2)}) copy-start(bf16[256,64]{0,1:T(8,128)(2,1)} %param.11) | copy-start | bytes 98308
  0.0 16.5 %copy-start.1 = (bf16[64,16,256]{2,1,0:T(8,128)(2,1)S(1)}, bf16[64,16,256]{2,1,0:T(8,128)(2,1)}, u32[]{:S(2)}) copy-start(bf16[64,16,256]{2,1,0:T(8,128)(2,1)} %param.9) | copy-start | bytes 1572868
  0.0 1.5 %collective-permute-start = (bf16[1,16,256]{2,1,0:T(8,128)(2,1)}, bf16[1,16,256]{2,1,0:T(8,128)(2,1)S(1)}, u32[]{:S(2)}, u32[]{:S(2)}) collective-permute-start(bf16[1,16,256]{2,1,0:T(8,128)(2,1)} %bitcast.137), channel_id=1, source_target_pairs={{0,1},{1,0},{2,3},{3,2},{4,5},{5,4},{6,7},{7,6},{8,9},{9,8},{10,11... | collective-permute-start | bytes 24584 | tf_op jit(solution)/shard_map/ppermute | solution.py:21
  2.2 4.6 %collective-permute-start.1 = (bf16[2,16,256]{2,1,0:T(8,128)(2,1)S(1)}, bf16[2,16,256]{2,1,0:T(8,128)(2,1)S(1)}, u32[]{:S(2)}, u32[]{:S(2)}) collective-permute-start(bf16[2,16,256]{2,1,0:T(8,128)(2,1)S(1)} %get-tuple-element.26), channel_id=1, source_target_pairs={{0,2},{1,3},{2,0},{3,1},{4,6},{5,7},{6,4},{7,5},{8,10},{9,11},{10,... | collective-permute-start | bytes 49160 | tf_op jit(solution)/shard_map/ppermute | solution.py:21
  6.9 4.1 %collective-permute-start.2 = (bf16[4,16,256]{2,1,0:T(8,128)(2,1)S(1)}, bf16[4,16,256]{2,1,0:T(8,128)(2,1)S(1)}, u32[]{:S(2)}, u32[]{:S(2)}) collective-permute-start(bf16[4,16,256]{2,1,0:T(8,128)(2,1)S(1)} %bitcast.133), channel_id=1, source_target_pairs={{0,4},{1,5},{2,6},{3,7},{4,0},{5,1},{6,2},{7,3},{8,12},{9,13},{10,... | collective-permute-start | bytes 98312 | tf_op jit(solution)/shard_map/ppermute | solution.py:21
  10.9 8.5 %copy-start.2 = (bf16[9,64,64]{2,1,0:T(8,128)(2,1)S(1)}, bf16[9,64,64]{2,1,0:T(8,128)(2,1)}, u32[]{:S(2)}) copy-start(bf16[9,64,64]{2,1,0:T(8,128)(2,1)} %param.12) | copy-start | bytes 221188
  11.0 5.3 %collective-permute-start.3 = (bf16[8,16,256]{2,1,0:T(8,128)(2,1)S(1)}, bf16[8,16,256]{2,1,0:T(8,128)(2,1)S(1)}, u32[]{:S(2)}, u32[]{:S(2)}) collective-permute-start(bf16[8,16,256]{2,1,0:T(8,128)(2,1)S(1)} %bitcast.131), channel_id=1, source_target_pairs={{0,8},{1,9},{2,10},{3,11},{4,12},{5,13},{6,14},{7,15},{8,0},{9,1},... | collective-permute-start | bytes 196616 | tf_op jit(solution)/shard_map/ppermute | solution.py:21
  16.8 2.9 %collective-permute-start.4 = (bf16[64,8,256]{2,0,1:T(8,128)(2,1)S(1)}, bf16[64,8,256]{2,0,1:T(8,128)(2,1)S(1)}, u32[]{:S(2)}, u32[]{:S(2)}) collective-permute-start(bf16[64,8,256]{2,0,1:T(8,128)(2,1)S(1)} %get-tuple-element.23), channel_id=1, source_target_pairs={{0,1},{1,2},{2,3},{3,4},{4,5},{5,6},{6,7},{7,8},{8,9},{9,10},{10,1... | collective-permute-start | bytes 786440 | tf_op jit(solution)/shard_map/ppermute | solution.py:40
  18.2 5.5 %collective-permute-start.5 = (bf16[64,8,256]{2,0,1:T(8,128)(2,1)S(1)}, bf16[64,8,256]{2,0,1:T(8,128)(2,1)S(1)}, u32[]{:S(2)}, u32[]{:S(2)}) collective-permute-start(bf16[64,8,256]{2,0,1:T(8,128)(2,1)S(1)} %get-tuple-element.24), channel_id=1, source_target_pairs={{1,0},{2,1},{3,2},{4,3},{5,4},{6,5},{7,6},{8,7},{9,8},{10,9},{11,1... | collective-permute-start | bytes 786440 | tf_op jit(solution)/shard_map/ppermute | solution.py:42
  24.0 2.0 %collective-permute-start.6 = (bf16[64,32,8]{2,0,1:T(8,128)(2,1)S(1)}, bf16[64,32,8]{2,0,1:T(8,128)(2,1)S(1)}, u32[]{:S(2)}, u32[]{:S(2)}) collective-permute-start(bf16[64,32,8]{2,0,1:T(8,128)(2,1)S(1)} %get-tuple-element.19), channel_id=1, source_target_pairs={} | collective-permute-start | bytes 98312 | tf_op jit(solution)/shard_map/ppermute | solution.py:40
  24.7 1.3 collective-permute-start.7
  29.0 35.4 %copy-start.4 = (f32[2,64]{1,0:T(2,128)S(1)}, f32[2,64]{1,0:T(2,128)}, u32[]{:S(2)}) copy-start(f32[2,64]{1,0:T(2,128)} %param.14) | copy-start | bytes 1540
  29.7 38.0 %copy-start.3 = (bf16[9,64,64]{2,1,0:T(8,128)(2,1)S(1)}, bf16[9,64,64]{2,1,0:T(8,128)(2,1)}, u32[]{:S(2)}) copy-start(bf16[9,64,64]{2,1,0:T(8,128)(2,1)} %param.13) | copy-start | bytes 221188
  65.1 2.9 %collective-permute-start.8 = (bf16[64,8,256]{2,0,1:T(8,128)(2,1)S(1)}, bf16[64,8,256]{2,0,1:T(8,128)(2,1)S(1)}, u32[]{:S(2)}, u32[]{:S(2)}) collective-permute-start(bf16[64,8,256]{2,0,1:T(8,128)(2,1)S(1)} %get-tuple-element.21), channel_id=1, source_target_pairs={{0,1},{1,2},{2,3},{3,4},{4,5},{5,6},{6,7},{7,8},{8,9},{9,10},{10,1... | collective-permute-start | bytes 786440 | tf_op jit(solution)/shard_map/ppermute | solution.py:40
  66.4 3.4 %collective-permute-start.9 = (bf16[64,8,256]{2,0,1:T(8,128)(2,1)S(1)}, bf16[64,8,256]{2,0,1:T(8,128)(2,1)S(1)}, u32[]{:S(2)}, u32[]{:S(2)}) collective-permute-start(bf16[64,8,256]{2,0,1:T(8,128)(2,1)S(1)} %get-tuple-element.22), channel_id=1, source_target_pairs={{1,0},{2,1},{3,2},{4,3},{5,4},{6,5},{7,6},{8,7},{9,8},{10,9},{11,1... | collective-permute-start | bytes 786440 | tf_op jit(solution)/shard_map/ppermute | solution.py:42
  70.2 1.9 %collective-permute-start.10 = (bf16[64,32,8]{2,0,1:T(8,128)(2,1)S(1)}, bf16[64,32,8]{2,0,1:T(8,128)(2,1)S(1)}, u32[]{:S(2)}, u32[]{:S(2)}) collective-permute-start(bf16[64,32,8]{2,0,1:T(8,128)(2,1)S(1)} %get-tuple-element.15), channel_id=1, source_target_pairs={} | collective-permute-start | bytes 98312 | tf_op jit(solution)/shard_map/ppermute | solution.py:40
  70.9 1.3 collective-permute-start.11
